TPU v7x, 32 devices: a whole 2x2x4 slice. The times are simulated.
32 devices in a mesh: dp: 4 (over x, y), tp: 8 (over z, core).
Axes of the slice: x: 2, y: 2, z: 4, core: 2. Of those that a mesh axis runs over, the one named last changes fastest.
Arguments:
- x: bfloat16 [512, 12288], P('dp'), parts along dimension 0
- w_gate: bfloat16 [12288, 33792], P(None, 'tp')
- w_up: bfloat16 [12288, 33792], P(None, 'tp')
- w_down: bfloat16 [33792, 12288], P('tp')
Outputs:
- output: bfloat16 [512, 12288], P('dp'), parts along dimension 0
There are 4 independent parts. A program takes and returns all parts, laid end to end along the dimension named above; an argument that names none is the same for every part.
All inputs are finite; a program needn't handle non-finite values.
Results may differ from a plain program's by a relative error of at most 0.016.
Values are sent between devices in bfloat16 or wider.
A program may use at most 2 GiB of HBM per device.

v0:
```python
import jax
import jax.numpy as jnp
from jax import lax
from jax.sharding import PartitionSpec as P


def solution(mesh):
    def step(x, w_gate, w_up, w_down):
        gate = jnp.dot(x, w_gate, preferred_element_type=jnp.float32)
        up = jnp.dot(x, w_up, preferred_element_type=jnp.float32)
        hidden = (jax.nn.silu(gate) * up).astype(jnp.bfloat16)
        term = jnp.dot(hidden, w_down, preferred_element_type=jnp.float32).astype(jnp.bfloat16)
        return lax.psum(term, "tp")

    return jax.shard_map(
        step,
        mesh=mesh,
        in_specs=(P("dp", None), P(None, "tp"), P(None, "tp"), P("tp", None)),
        out_specs=P("dp", None),
        check_vma=False,
    )
```

profile of v0, /device:TPU:1, one launch (start us, length us, event | category | flops | bytes accessed | tf_op | source)
XLA Modules:
  0.0 205.6 jit_solution(8380778642292433408)
XLA Ops:
  6.5 0.0 copy-start
  6.5 0.0 all-reduce.2.cloned.1.call-start
  6.5 1.9 copy-done
  8.4 35.8 %fusion.1 = f32[128,4224]{1,0:T(8,128)} fusion(bf16[128,12288]{1,0:T(8,128)(2,1)S(1)} %copy-done, bf16[12288,4224]{1,0:T(8,128)(2,1)} %param.5), kind=kOutput, calls=%fused_computation.3 | convolution fusion | flops 13287555072 | bytes 109117440 | tf_op jit(solution)/shard_map/dot_general | solution.py:9
  44.2 35.6 %fusion = bf16[128,4224]{1,0:T(8,128)(2,1)} fusion(bf16[128,12288]{1,0:T(8,128)(2,1)S(1)} %copy-done, bf16[12288,4224]{1,0:T(8,128)(2,1)} %param.6, f32[128,4224]{1,0:T(8,128)} %fusion.1), kind=kOutput, calls=%fused_computation.2 | convolution fusion | flops 13290799104 | bytes 110198784 | tf_op jit(solution)/shard_map/dot_general | solution.py:10
  79.9 36.4 %convolution_convert_fusion = bf16[128,12288]{1,0:T(8,128)(2,1)} fusion(bf16[128,4224]{1,0:T(8,128)(2,1)} %fusion, bf16[4224,12288]{1,0:T(8,128)(2,1)} %param.7), kind=kOutput, calls=%fused_computation | convolution fusion | flops 13289127936 | bytes 108036096 | tf_op jit(solution)/shard_map/dot_general | solution.py:12
  116.3 0.0 all-reduce.2.cloned.1.call-update
  116.3 78.6 %all-reduce.2.cloned.1.call-done = bf16[128,12288]{1,0:T(8,128)(2,1)} async-done(((bf16[128,12288]{1,0:T(8,128)(2,1)}), bf16[128,12288]{1,0:T(8,128)(2,1)}) %all-reduce.2.cloned.1.call-update) | async-done | bytes 3145744 | tf_op jit(solution)/shard_map/psum | solution.py:13
  195.0 3.8 %copy.6 = bf16[128,12288]{1,0:T(8,128)(2,1)} copy(bf16[128,12288]{1,0:T(8,128)(2,1)} %all-reduce.2.cloned.1.call-done) | data formatting | bytes 6291456
Async XLA Ops:
  6.5 1.9 copy-start
  6.5 188.4 %all-reduce.2.cloned.1.call-start = ((), (), s32[]{:S(2)}) async-start(), calls=%async_computation | async-start | bytes 6291456 | tf_op jit(solution)/shard_map/psum | solution.py:13
Sparse Core Ops, SparseCore 0:
  116.5 78.4 all-reduce.1
where the time goes:
time: 207 us; the launch traced here: 206 us
  matrix products  108 us (52%)
  waiting for transfers between devices  78.6 us (38%)
  between operations  13.4 us (6%)
  local copies, waits for them, and re-layouts  5.72 us (3%)
    psum x1, waiting for transfers between devices, step(): return lax.psum(term, 'tp')  78.6 us
    dot_general x1, matrix products, step(): jnp.dot(hidden, w_down, preferred_element_type=jnp.float32)  36.4 us
    dot_general x1, matrix products, step(): gate = jnp.dot(x, w_gate, preferred_element_type=jnp.float32)  35.8 us
    dot_general x1, matrix products, step(): up = jnp.dot(x, w_up, preferred_element_type=jnp.float32)  35.6 us
    unnamed x3, local copies, waits for them, and re-layouts  5.72 us
  transfers between devices with their start and end apart: 1, of which 1 were waited for; matrix products, arithmetic and copies ran while one was open for 0% of the time, Pallas kernels for 0%

commit v1 on v0

v1 whole, which is shorter than its diff:
```python
import functools

import jax
import jax.numpy as jnp
from jax import lax
from jax.experimental import pallas as pl
from jax.experimental.pallas import tpu as pltpu
from jax.sharding import PartitionSpec as P

MESH = pl.DeviceIdType.MESH
BF16, F32 = jnp.bfloat16, jnp.float32
LANES = 128

KC = 512
NS = 4
CW = 512
ND = 4
RING = 12
LD, LX, LE, LR, LF, LY = 1, 3, 5, 7, 9, 10


def kernel(
    rows, depth, units, kc, cw,
    x_hbm, wg_hbm, wu_hbm, wd_hbm, y_hbm,
    xs, wbuf, acc, hid, dbuf, held, d_out, d_in, x_out, x_in, e_out, e_in, r_out, r_in, yv,
    xl_sem, w_sem, wd_sem, y_sem, send_sem, xa_sem, xb_sem, d_sem, x_sem, z_sem, y_in_sem,
):
    dp, tp = lax.axis_index("dp"), lax.axis_index("tp")
    z, core = tp // 2, tp % 2
    side = dp // 2
    across = (dp + 2) % 4
    partner = tp + 1 - 2 * core
    is_end = (z == 0) | (z == 3)
    is_mid = (z == 1) | (z == 2)
    half = z // 2
    z_end, z_far = 3 * half, 2 - half
    z_mid = 1 + half
    tp_end, tp_far, tp_mid = z_end * 2 + core, z_far * 2 + core, z_mid * 2 + core

    nk, nch = depth // kc, depth // cw
    tiles = units // LANES
    wt = (tiles + 1) // 2
    width = wt * LANES
    first = pl.multiple_of(side * ((tiles - wt) * LANES), LANES)
    hc, qc = cw // 2, cw // 4
    own, oth = pl.ds(0, rows), pl.ds(rows, rows)

    def weights(k):
        slot = lax.rem(k, NS)
        r = pl.ds(pl.multiple_of(k * kc, kc), kc)
        c = pl.ds(first, width)
        return (
            pltpu.make_async_copy(wg_hbm.at[r, c], wbuf.at[slot, :, pl.ds(0, width)], w_sem.at[slot, 0]),
            pltpu.make_async_copy(wu_hbm.at[r, c], wbuf.at[slot, :, pl.ds(width, width)], w_sem.at[slot, 1]),
        )

    def down(n):
        slot = lax.rem(n, ND)
        r = pl.ds(first, width)
        mine = pl.ds(pl.multiple_of(n * cw + core * hc, LANES), hc)
        others = pl.ds(pl.multiple_of(n * cw + (1 - core) * hc, LANES), hc)
        return (
            pltpu.make_async_copy(wd_hbm.at[r, mine], dbuf.at[slot, :, pl.ds(0, hc)], wd_sem.at[slot, 0]),
            pltpu.make_async_copy(wd_hbm.at[r, others], dbuf.at[slot, :, pl.ds(hc, hc)], wd_sem.at[slot, 1]),
        )

    def send(src, dst, kind, recv, **where):
        return pltpu.make_async_remote_copy(
            src_ref=src, dst_ref=dst, send_sem=send_sem.at[kind], recv_sem=recv,
            device_id=where, device_id_type=MESH,
        )

    def x_piece(k, c):
        return pl.ds(pl.multiple_of(k * kc + c * (kc // 2), LANES), kc // 2)

    def x_across(k):
        cols = x_piece(k, core)
        return send(x_hbm.at[:, cols], xs.at[oth, cols], 0, xa_sem.at[k], dp=across)

    def x_partner(k, c):
        cols = x_piece(k, c)
        return send(xs.at[oth, cols], xs.at[oth, cols], 1, xb_sem.at[k], tp=partner)

    def d_copy(n):
        return send(d_out.at[n], d_in.at[n], 2, d_sem.at[n], tp=partner)

    def x_copy(n):
        return send(x_out.at[n], x_in.at[n], 3, x_sem.at[n], dp=across)

    def e_copy(n):
        return send(e_out.at[n], e_in.at[n], 4, z_sem.at[0, n], tp=tp_mid)

    def r_copy(n):
        return send(r_out.at[n], r_in.at[n], 5, z_sem.at[1, n], tp=tp_far)

    def y_half(n, h):
        return pl.ds(pl.multiple_of(n * cw + core * hc + h * qc, LANES), qc)

    def f_far(n, h):
        c = y_half(n, h)
        return send(yv.at[:, c], yv.at[:, c], 6, z_sem.at[2, n], tp=tp_far)

    def f_end(n, h):
        c = y_half(n, h)
        return send(yv.at[:, c], yv.at[:, c], 7, z_sem.at[0, n], tp=tp_end)

    def g_end(n, h):
        c = y_half(n, h)
        return send(yv.at[:, c], yv.at[:, c], 8, z_sem.at[1, n], tp=tp_end)

    def y_core(n, c):
        return pl.ds(pl.multiple_of(n * cw + c * hc, LANES), hc)

    def y_partner(n, c):
        cols = y_core(n, c)
        return send(yv.at[:, cols], yv.at[:, cols], 9, y_in_sem.at[n], tp=partner)

    def y_store(n):
        cols = pl.ds(pl.multiple_of(n * cw, LANES), cw)
        return pltpu.make_async_copy(yv.at[:, cols], y_hbm.at[:, cols], y_sem)

    x_local = pltpu.make_async_copy(x_hbm, xs.at[own, :], xl_sem)
    x_local.start()
    for k in range(NS):
        for c in weights(k):
            c.start()
    barrier = pltpu.get_barrier_semaphore()
    pl.semaphore_signal(barrier, inc=1, device_id={"dp": across}, device_id_type=MESH)
    pl.semaphore_signal(barrier, inc=1, device_id={"tp": partner}, device_id_type=MESH)

    @pl.when(is_end)
    def _():
        pl.semaphore_signal(barrier, inc=1, device_id={"tp": tp_mid}, device_id_type=MESH)
        pl.semaphore_wait(barrier, 3)

    @pl.when(is_mid)
    def _():
        pl.semaphore_signal(barrier, inc=1, device_id={"tp": tp_end}, device_id_type=MESH)
        pl.semaphore_signal(barrier, inc=1, device_id={"tp": tp_far}, device_id_type=MESH)
        pl.semaphore_wait(barrier, 4)

    @pl.loop(0, nk)
    def _(k):
        x_across(k).start()

    for n in range(ND):
        for c in down(n):
            c.start()

    @pl.loop(0, 2 * wt)
    def _(j):
        acc[:, pl.ds(pl.multiple_of(j * LANES, LANES), LANES)] = jnp.zeros((2 * rows, LANES), F32)

    x_local.wait()
    x_across(0).wait_recv()
    x_partner(0, core).start()

    @pl.loop(0, nk)
    def _(k):
        slot = lax.rem(k, NS)

        @pl.when(k + 1 < nk)
        def _():
            x_across(k + 1).wait_recv()
            x_partner(k + 1, core).start()

        for c in weights(k):
            c.wait()
        x_partner(k, 1 - core).wait_recv()
        cols = pl.ds(pl.multiple_of(k * kc, kc), kc)
        for t in range(0, 2 * wt, 2):
            out = pl.ds(t * LANES, 2 * LANES)
            acc[:, out] += jnp.dot(xs[:, cols], wbuf[slot, :, out], preferred_element_type=F32)

        @pl.when(k + NS < nk)
        def _():
            for c in weights(k + NS):
                c.start()

    def hidden(j):
        g = acc[:, pl.ds(pl.multiple_of(j * LANES, LANES), LANES)]
        u = acc[:, pl.ds(pl.multiple_of(width + j * LANES, LANES), LANES)]
        return (g * jax.nn.sigmoid(g) * u).astype(BF16)

    @pl.loop(0, wt)
    def _(j):
        hid[:, pl.ds(pl.multiple_of(j * LANES, LANES), LANES)] = hidden(j)

    if tiles % 2:
        @pl.when(side == 1)
        def _():
            hid[:, pl.ds(0, LANES)] = jnp.zeros((2 * rows, LANES), BF16)

    @pl.loop(0, nch + LY)
    def _(it):
        @pl.when(it < nch)
        def _():
            slot = lax.rem(it, ND)
            for c in down(it):
                c.wait()
            held[lax.rem(it, RING)] = jnp.dot(hid[...], dbuf[slot, :, :hc], preferred_element_type=F32)
            d_out[it] = jnp.dot(hid[...], dbuf[slot, :, hc:], preferred_element_type=F32).astype(BF16)
            d_copy(it).start()

            @pl.when(it + ND < nch)
            def _():
                for c in down(it + ND):
                    c.start()

        def stage(lag):
            return (it >= lag) & (it < nch + lag)

        @pl.when(stage(LD))
        def _():
            n = it - LD
            at = lax.rem(n, RING)
            d_copy(n).wait_recv()
            held[at, own, :] += d_in[n, own, :].astype(F32)
            x_out[n] = (held[at, oth, :] + d_in[n, oth, :].astype(F32)).astype(BF16)
            x_copy(n).start()

        @pl.when(stage(LX))
        def _():
            n = it - LX
            at = lax.rem(n, RING)
            x_copy(n).wait_recv()
            total = held[at, own, :] + x_in[n].astype(F32)

            @pl.when(is_end)
            def _():
                e_out[n] = total.astype(BF16)
                e_copy(n).start()

            @pl.when(is_mid)
            def _():
                held[at, own, :] = total

        @pl.when(stage(LE) & is_mid)
        def _():
            n = it - LE
            at = lax.rem(n, RING)
            e_copy(n).wait_recv()
            total = held[at, own, :] + e_in[n].astype(F32)
            low, high = total[:, :qc], total[:, qc:]
            r_out[n] = jnp.where(half == 0, high, low).astype(BF16)
            held[at, own, pl.ds(0, qc)] = jnp.where(half == 0, low, high)
            r_copy(n).start()

        @pl.when(stage(LR) & is_mid)
        def _():
            n = it - LR
            at = lax.rem(n, RING)
            r_copy(n).wait_recv()
            yv[:, y_half(n, half)] = (held[at, own, pl.ds(0, qc)] + r_in[n].astype(F32)).astype(BF16)
            f_far(n, half).start()
            f_end(n, half).start()

        @pl.when(stage(LF))
        def _():
            n = it - LF

            @pl.when(is_mid)
            def _():
                f_far(n, 1 - half).wait_recv()
                g_end(n, 1 - half).start()

            @pl.when(is_end)
            def _():
                f_end(n, half).wait_recv()
                g_end(n, 1 - half).wait_recv()

            y_partner(n, core).start()

        @pl.when(stage(LY))
        def _():
            n = it - LY
            y_partner(n, 1 - core).wait_recv()
            y_store(n).start()

    half_x = pl.ds(0, depth // 2)
    quarter = pl.ds(0, depth // 4)

    def drain(ref, kind):
        send(ref, ref, kind, xl_sem, tp=partner).wait_send()

    drain(xs.at[own, half_x], 0)
    drain(xs.at[own, half_x], 1)
    drain(d_out, 2)
    drain(x_out, 3)

    @pl.when(is_end)
    def _():
        drain(e_out, 4)

    @pl.when(is_mid)
    def _():
        drain(r_out, 5)
        for kind in (6, 7, 8):
            drain(yv.at[:, quarter], kind)

    drain(yv.at[:, half_x], 9)
    pltpu.make_async_copy(yv, y_hbm, y_sem).wait()


def solution(mesh):
    def step(x, w_gate, w_up, w_down):
        rows, depth = x.shape
        units = w_gate.shape[1]
        kc, cw = KC, CW
        wt = (units // LANES + 1) // 2
        width = wt * LANES
        nk, nch = depth // kc, depth // cw
        hc, qc = cw // 2, cw // 4
        dma = pltpu.SemaphoreType.DMA
        return pl.pallas_call(
            functools.partial(kernel, rows, depth, units, kc, cw),
            out_shape=jax.ShapeDtypeStruct((rows, depth), BF16),
            in_specs=[pl.BlockSpec(memory_space=pl.ANY)] * 4,
            out_specs=pl.BlockSpec(memory_space=pl.ANY),
            scratch_shapes=[
                pltpu.VMEM((2 * rows, depth), BF16),
                pltpu.VMEM((NS, kc, 2 * width), BF16),
                pltpu.VMEM((2 * rows, 2 * width), F32),
                pltpu.VMEM((2 * rows, width), BF16),
                pltpu.VMEM((ND, width, cw), BF16),
                pltpu.VMEM((RING, 2 * rows, hc), F32),
                pltpu.VMEM((nch, 2 * rows, hc), BF16),
                pltpu.VMEM((nch, 2 * rows, hc), BF16),
                pltpu.VMEM((nch, rows, hc), BF16),
                pltpu.VMEM((nch, rows, hc), BF16),
                pltpu.VMEM((nch, rows, hc), BF16),
                pltpu.VMEM((nch, rows, hc), BF16),
                pltpu.VMEM((nch, rows, qc), BF16),
                pltpu.VMEM((nch, rows, qc), BF16),
                pltpu.VMEM((rows, depth), BF16),
                dma,
                dma((NS, 2)),
                dma((ND, 2)),
                dma,
                dma((10,)),
                dma((nk,)),
                dma((nk,)),
                dma((nch,)),
                dma((nch,)),
                dma((3, nch)),
                dma((nch,)),
            ],
            compiler_params=pltpu.CompilerParams(
                collective_id=0, has_side_effects=True, vmem_limit_bytes=66_000_000
            ),
        )(x, w_gate, w_up, w_down)

    return jax.shard_map(
        step,
        mesh=mesh,
        in_specs=(P("dp", None), P(None, "tp"), P(None, "tp"), P("tp", None)),
        out_specs=P("dp", None),
        check_vma=False,
    )
```

time: 207 us -> 125 us (0.60)
  Pallas kernels: 0 us -> 121 us
  matrix products: 108 us -> 0 us
  waiting for transfers between devices: 78.6 us -> 0 us
  between operations: 13.4 us -> 0.01 us
    pallas_call x0 -> x1, Pallas kernels: none -> 121 us  [step(): pl.pallas_call(functools.partial(kernel, rows, depth, units, kc, cw), out...]
    dot_general x3 -> x0, matrix products: 108 us -> none  [the longest x1 36.4 us: step(): jnp.dot(hidden, w_down, preferred_element_type=jnp.float32)]
    psum x1 -> x0, waiting for transfers between devices: 78.6 us -> none  [step(): return lax.psum(term, 'tp')]
    unnamed x3 -> x1, local copies, waits for them, and re-layouts: 5.72 us -> 3.83 us
  transfers between devices with their start and end apart: 1 -> 0, of which waited for: 1 -> 0; matrix products, arithmetic and copies ran while one was open for 0% -> 0% of each run, Pallas kernels for 0% -> 0%
where the time goes in v1:
time: 125 us
  Pallas kernels  121 us (97%)
  local copies, waits for them, and re-layouts  3.83 us (3%)
    pallas_call x1, Pallas kernels, step(): pl.pallas_call(functools.partial(kernel, rows, depth, units, kc, cw), out...  121 us
    unnamed x1, local copies, waits for them, and re-layouts  3.83 us

profile of v1, /device:TPU:1, one launch (start us, length us, event | category | flops | bytes accessed | tf_op | source)
XLA Modules:
  0.0 125.3 jit_solution(9422054565947429890)
XLA Ops:
  0.0 121.4 %shard_map.46 = bf16[128,12288]{1,0:T(8,128)(2,1)} custom-call(bf16[128,12288]{1,0:T(8,128)(2,1)} %x_hbm.1, bf16[12288,4224]{1,0:T(8,128)(2,1)} %wg_hbm.1, bf16[12288,4224]{1,0:T(8,128)(2,1)} %wu_hbm.1, bf16[4224,12288]{1,0:T(8,128)(2,1)} %wd_hbm.1), custom_call_target="tpu_custom_call" | custom-call | tf_op jit(solution)/shard_map/pallas_call | solution.py:315
  121.4 3.8 %copy.6 = bf16[128,12288]{1,0:T(8,128)(2,1)} copy(bf16[128,12288]{1,0:T(8,128)(2,1)} %shard_map.46) | data formatting | bytes 6291456

commit v2 on v0

v2 whole, which is shorter than its diff:
```python
import functools

import jax
import jax.numpy as jnp
from jax import lax
from jax.experimental import pallas as pl
from jax.experimental.pallas import tpu as pltpu
from jax.sharding import PartitionSpec as P

MESH = pl.DeviceIdType.MESH
BF16, F32 = jnp.bfloat16, jnp.float32
LANES = 128

KC = 512
NS = 6
DIRECT = 2
CW = 512
SPLIT = 2
ND = 4
LD, LX, LE, LR, LG = 1, 4, 6, 9, 13

PARTS = 6


def kernel(
    rows, depth, units, kc, cw,
    x_hbm, wg_hbm, wu_hbm, wd_hbm, y_hbm,
    xs, wbuf, acc, hid, dbuf, d_in, x_in, e_in, r_in, yv,
    xl_sem, w_sem, wd_sem, y_sem, send_sem, xa_sem, xz_sem, xb_sem, d_sem, x_sem, z_sem, y_in_sem,
):
    dp, tp = lax.axis_index("dp"), lax.axis_index("tp")
    z, core = tp // 2, tp % 2
    side = dp // 2
    across = (dp + 2) % 4
    partner = tp + 1 - 2 * core
    is_end = (z == 0) | (z == 3)
    is_mid = (z == 1) | (z == 2)
    odd = z % 2
    tp_pair = tp + 2 - 4 * odd
    tp_far = (3 - z) * 2 + core

    nk, nch = depth // kc, depth // cw
    tiles = units // LANES
    wt = (tiles + 1) // 2
    width = wt * LANES
    first = pl.multiple_of(side * ((tiles - wt) * LANES), LANES)
    hc = cw // 2
    sc = hc // SPLIT
    ring = 2 * width // hc
    own, oth, both = pl.ds(0, rows), pl.ds(rows, rows), pl.ds(0, 2 * rows)

    def weights(k):
        slot = lax.rem(k, NS)
        r = pl.ds(pl.multiple_of(k * kc, kc), kc)
        c = pl.ds(first, width)
        return (
            pltpu.make_async_copy(wg_hbm.at[r, c], wbuf.at[slot, :, pl.ds(0, width)], w_sem.at[slot, 0]),
            pltpu.make_async_copy(wu_hbm.at[r, c], wbuf.at[slot, :, pl.ds(width, width)], w_sem.at[slot, 1]),
        )

    def down(n):
        slot = lax.rem(n, ND)
        r = pl.ds(first, width)
        mine = pl.ds(pl.multiple_of(n * cw + core * hc, LANES), hc)
        others = pl.ds(pl.multiple_of(n * cw + (1 - core) * hc, LANES), hc)
        return (
            pltpu.make_async_copy(wd_hbm.at[r, mine], dbuf.at[slot, :, pl.ds(0, hc)], wd_sem.at[slot, 0]),
            pltpu.make_async_copy(wd_hbm.at[r, others], dbuf.at[slot, :, pl.ds(hc, hc)], wd_sem.at[slot, 1]),
        )

    def send(src, dst, kind, recv, **where):
        return pltpu.make_async_remote_copy(
            src_ref=src, dst_ref=dst, send_sem=send_sem.at[kind], recv_sem=recv,
            device_id=where, device_id_type=MESH,
        )

    def x_half(k, c):
        return pl.ds(pl.multiple_of(k * kc + c * (kc // 2), LANES), kc // 2)

    def x_quarter(k, q):
        return pl.ds(pl.multiple_of(k * kc + core * (kc // 2) + q * (kc // 4), LANES), kc // 4)

    def x_whole(k):
        c = x_half(k, core)
        return send(xs.at[own, c], xs.at[oth, c], 0, xa_sem.at[k], dp=across)

    def x_part(k):
        c = x_quarter(k, odd)
        return send(xs.at[own, c], xs.at[oth, c], 0, xa_sem.at[k], dp=across)

    def x_pair(k, q):
        c = x_quarter(k, q)
        return send(xs.at[oth, c], xs.at[oth, c], 1, xz_sem.at[k], tp=tp_pair)

    def x_partner(k, c):
        c = x_half(k, c)
        return send(xs.at[oth, c], xs.at[oth, c], 2, xb_sem.at[k], tp=partner)

    def d_out(n):
        return wbuf.at[0, pl.ds((n % 2) * 256, 2 * rows), pl.ds(pl.multiple_of((n // 2) * hc, hc), hc)]

    def part(n, s):
        return pl.ds(pl.multiple_of((n // 2) * hc + s * sc, sc), sc)

    def x_out(n, s):
        return wbuf.at[1, pl.ds((n % 2) * 256, rows), part(n, s)]

    def z_out(n, s):
        return wbuf.at[2, pl.ds((n % 2) * 256, rows), part(n, s)]

    def d_copy(n):
        return send(d_out(n), d_in.at[n], 3, d_sem.at[n], tp=partner)

    def x_copy(n, s):
        m = n * SPLIT + s
        return send(x_out(n, s), x_in.at[m], 4, x_sem.at[m], dp=across)

    def e_copy(n, s):
        m = n * SPLIT + s
        return send(z_out(n, s), e_in.at[m], 5, z_sem.at[0, m], tp=tp_pair)

    def r_copy(n, s):
        m = n * SPLIT + s
        return send(z_out(n, s), r_in.at[m], 5, z_sem.at[1, m], tp=tp_far)

    def y_core(n, s, c):
        return pl.ds(pl.multiple_of(n * cw + c * hc + s * sc, LANES), sc)

    def g_copy(n, s):
        c = y_core(n, s, core)
        return send(yv.at[:, c], yv.at[:, c], 6, z_sem.at[0, n * SPLIT + s], tp=tp_pair)

    def y_partner(n, s, c):
        c = y_core(n, s, c)
        return send(yv.at[:, c], yv.at[:, c], 7, y_in_sem.at[n * SPLIT + s], tp=partner)

    def y_store(n):
        cols = pl.ds(pl.multiple_of(n * cw, LANES), cw)
        return pltpu.make_async_copy(yv.at[:, cols], y_hbm.at[:, cols], y_sem)

    x_local = pltpu.make_async_copy(x_hbm, xs.at[own, :], xl_sem)
    x_local.start()
    barrier = pltpu.get_barrier_semaphore()
    pl.semaphore_signal(barrier, inc=1, device_id={"dp": across}, device_id_type=MESH)
    pl.semaphore_signal(barrier, inc=1, device_id={"tp": partner}, device_id_type=MESH)
    pl.semaphore_signal(barrier, inc=1, device_id={"tp": tp_pair}, device_id_type=MESH)

    @pl.when(is_mid)
    def _():
        pl.semaphore_signal(barrier, inc=1, device_id={"tp": tp_far}, device_id_type=MESH)

    x_local.wait()
    for k in range(4):
        for c in weights(k):
            c.start()

    @pl.when(is_end)
    def _():
        pl.semaphore_wait(barrier, 3)

    @pl.when(is_mid)
    def _():
        pl.semaphore_wait(barrier, 4)

    @pl.loop(0, DIRECT)
    def _(k):
        x_whole(k).start()

    @pl.loop(DIRECT, nk)
    def _(k):
        x_part(k).start()

    @pl.loop(0, 2 * wt)
    def _(j):
        acc[:, pl.ds(pl.multiple_of(j * LANES, LANES), LANES)] = jnp.zeros((2 * rows, LANES), F32)

    def project(i, r):
        a, b = lax.rem(2 * i, NS), lax.rem(2 * i + 1, NS)
        ka = pl.ds(pl.multiple_of(2 * i * kc, kc), kc)
        kb = pl.ds(pl.multiple_of((2 * i + 1) * kc, kc), kc)

        def tile(r, t):
            out = pl.ds(t * LANES, 2 * LANES)
            acc[r, out] += jnp.dot(xs[r, ka], wbuf[a, :, out], preferred_element_type=F32) + jnp.dot(
                xs[r, kb], wbuf[b, :, out], preferred_element_type=F32
            )

        for t in range(0, 2 * wt - 2, 2):
            tile(r, t)
        if r is both:
            tile(own, 2 * wt - 2)
            tile(oth, 2 * wt - 2)
        else:
            tile(r, 2 * wt - 2)

    def to_pair(k):
        k = jnp.int32(k)

        @pl.when((k >= DIRECT) & (k < nk))
        def _():
            x_part(k).wait_recv()
            x_pair(k, odd).start()

    def to_partner(k):
        k = jnp.int32(k)

        @pl.when(k < DIRECT)
        def _():
            x_whole(k).wait_recv()

        @pl.when((k >= DIRECT) & (k < nk))
        def _():
            x_pair(k, 1 - odd).wait_recv()

        @pl.when(k < nk)
        def _():
            x_partner(k, core).start()

    def pieces(i, per):
        for j in range(2):
            per(2 * i + j)

    def refill(i):
        for j in range(2):
            k = jnp.int32(2 * i + j + NS)

            @pl.when(k < nk)
            def _():
                for c in weights(k):
                    c.start()

            @pl.when((k >= nk) & (k < nk + ND))
            def _():
                for c in down(k - nk):
                    c.start()

    def early(i, r):
        for k in (2 * i, 2 * i + 1):
            if r is own:
                for c in weights(k):
                    c.wait()
                if i == 0:
                    for c in weights(k + 4):
                        c.start()
            else:
                x_partner(k, 1 - core).wait_recv()
        project(i, r)
        if r is oth:
            refill(i)

    early(0, own)
    early(1, own)
    pieces(0, to_partner)
    pieces(1, to_pair)
    early(2, own)
    pieces(2, to_pair)
    early(0, oth)
    pieces(3, to_pair)
    pieces(1, to_partner)
    pieces(4, to_pair)
    pieces(2, to_partner)
    early(1, oth)
    pieces(5, to_pair)
    pieces(3, to_partner)
    early(2, oth)

    @pl.loop(3, nk // 2)
    def _(i):
        pieces(i + 3, to_pair)
        pieces(i + 1, to_partner)
        for j in range(2):
            for c in weights(2 * i + j):
                c.wait()
            x_partner(2 * i + j, 1 - core).wait_recv()
        project(i, both)
        refill(i)

    @pl.loop(0, wt)
    def _(j):
        g = acc[:, pl.ds(pl.multiple_of(j * LANES, LANES), LANES)]
        u = acc[:, pl.ds(pl.multiple_of(width + j * LANES, LANES), LANES)]
        hid[:, pl.ds(pl.multiple_of(j * LANES, LANES), LANES)] = (g * jax.nn.sigmoid(g) * u).astype(BF16)

    if tiles % 2:
        @pl.when(side == 1)
        def _():
            hid[:, pl.ds(0, LANES)] = jnp.zeros((2 * rows, LANES), BF16)

    def held(n):
        return pl.ds(pl.multiple_of(lax.rem(n, ring) * hc, hc), hc)

    def held_part(n, s):
        return pl.ds(pl.multiple_of(lax.rem(n, ring) * hc + s * sc, sc), sc)

    @pl.loop(0, nch + LG + 1)
    def _(it):
        @pl.when(it < nch)
        def _():
            slot = lax.rem(it, ND)
            for c in down(it):
                c.wait()
            term = jnp.dot(hid[...], dbuf[slot], preferred_element_type=F32)
            acc[:, held(it)] = term[:, :hc]
            d_out(it)[...] = term[:, hc:].astype(BF16)
            d_copy(it).start()

            @pl.when(it + ND < nch)
            def _():
                for c in down(it + ND):
                    c.start()

        def stage(lag):
            return (it >= lag) & (it < nch + lag)

        @pl.when(stage(LD))
        def _():
            n = it - LD
            d_copy(n).wait_recv()
            for s in range(SPLIT):
                got = pl.ds(s * sc, sc)
                x_out(n, s)[...] = (acc[oth, held_part(n, s)] + d_in[n, oth, got].astype(F32)).astype(BF16)
                x_copy(n, s).start()
            acc[own, held(n)] += d_in[n, own, :].astype(F32)

        @pl.when(stage(LX))
        def _():
            n = it - LX
            for s in range(SPLIT):
                at = held_part(n, s)
                x_copy(n, s).wait_recv()
                total = acc[own, at] + x_in[n * SPLIT + s].astype(F32)

                @pl.when(is_end)
                def _():
                    z_out(n, s)[...] = total.astype(BF16)
                    e_copy(n, s).start()

                @pl.when(is_mid)
                def _():
                    acc[own, at] = total

        @pl.when(stage(LE) & is_mid)
        def _():
            n = it - LE
            for s in range(SPLIT):
                e_copy(n, s).wait_recv()
                total = acc[own, held_part(n, s)] + e_in[n * SPLIT + s].astype(F32)
                z_out(n, s)[...] = total.astype(BF16)
                r_copy(n, s).start()

        @pl.when(stage(LR) & is_mid)
        def _():
            n = it - LR
            for s in range(SPLIT):
                r_copy(n, s).wait_recv()
                total = z_out(n, s)[...].astype(F32) + r_in[n * SPLIT + s].astype(F32)
                yv[:, y_core(n, s, core)] = total.astype(BF16)
                g_copy(n, s).start()
                y_partner(n, s, core).start()

        @pl.when(stage(LG) & is_end)
        def _():
            n = it - LG
            for s in range(SPLIT):
                g_copy(n, s).wait_recv()
                y_partner(n, s, core).start()

        last = jnp.where(is_mid, LR, LG) + 1

        @pl.when(stage(last))
        def _():
            n = it - last
            for s in range(SPLIT):
                y_partner(n, s, 1 - core).wait_recv()
            y_store(n).start()

    def drain(kind, columns):
        ref = yv.at[:, pl.ds(0, columns)]
        send(ref, ref, kind, xl_sem, tp=partner).wait_send()

    drain(0, DIRECT * (kc // 2) + (nk - DIRECT) * (kc // 4))
    drain(1, (nk - DIRECT) * (kc // 4))
    drain(2, depth // 2)
    drain(3, depth)
    drain(4, depth // 2)
    drain(5, depth // 2)

    @pl.when(is_mid)
    def _():
        drain(6, depth // 2)

    drain(7, depth // 2)
    pltpu.make_async_copy(yv, y_hbm, y_sem).wait()


def hand_on(y_hbm, out_hbm, buf, in_sem, out_sem):
    columns = y_hbm.shape[1] // PARTS
    cols = [pl.ds(j * columns, columns) for j in range(PARTS)]
    for j, c in enumerate(cols):
        pltpu.make_async_copy(y_hbm.at[:, c], buf.at[:, c], in_sem.at[j]).start()
    for j, c in enumerate(cols):
        pltpu.make_async_copy(y_hbm.at[:, c], buf.at[:, c], in_sem.at[j]).wait()
        pltpu.make_async_copy(buf.at[:, c], out_hbm.at[:, c], out_sem.at[j]).start()
    for j, c in enumerate(cols):
        pltpu.make_async_copy(buf.at[:, c], out_hbm.at[:, c], out_sem.at[j]).wait()


def solution(mesh):
    def step(x, w_gate, w_up, w_down):
        rows, depth = x.shape
        units = w_gate.shape[1]
        kc, cw = KC, CW
        wt = (units // LANES + 1) // 2
        width = wt * LANES
        nk, nch = depth // kc, depth // cw
        hc = cw // 2
        dma = pltpu.SemaphoreType.DMA
        y = pl.pallas_call(
            functools.partial(kernel, rows, depth, units, kc, cw),
            out_shape=jax.ShapeDtypeStruct((rows, depth), BF16),
            in_specs=[pl.BlockSpec(memory_space=pl.ANY)] * 4,
            out_specs=pl.BlockSpec(memory_space=pl.ANY),
            scratch_shapes=[
                pltpu.VMEM((2 * rows, depth), BF16),
                pltpu.VMEM((NS, kc, 2 * width), BF16),
                pltpu.VMEM((2 * rows, 2 * width), F32),
                pltpu.VMEM((2 * rows, width), BF16),
                pltpu.VMEM((ND, width, cw), BF16),
                pltpu.VMEM((nch, 2 * rows, hc), BF16),
                pltpu.VMEM((nch * SPLIT, rows, hc // SPLIT), BF16),
                pltpu.VMEM((nch * SPLIT, rows, hc // SPLIT), BF16),
                pltpu.VMEM((nch * SPLIT, rows, hc // SPLIT), BF16),
                pltpu.VMEM((rows, depth), BF16),
                dma,
                dma((NS, 2)),
                dma((ND, 2)),
                dma,
                dma((8,)),
                dma((nk,)),
                dma((nk,)),
                dma((nk,)),
                dma((nch,)),
                dma((nch * SPLIT,)),
                dma((2, nch * SPLIT)),
                dma((nch * SPLIT,)),
            ],
            compiler_params=pltpu.CompilerParams(
                collective_id=0, has_side_effects=True, vmem_limit_bytes=66_000_000
            ),
        )(x, w_gate, w_up, w_down)
        return pl.pallas_call(
            hand_on,
            out_shape=jax.ShapeDtypeStruct((rows, depth), BF16),
            in_specs=[pl.BlockSpec(memory_space=pl.ANY)],
            out_specs=pl.BlockSpec(memory_space=pl.ANY),
            scratch_shapes=[pltpu.VMEM((rows, depth), BF16), dma((PARTS,)), dma((PARTS,))],
        )(y)

    return jax.shard_map(
        step,
        mesh=mesh,
        in_specs=(P("dp", None), P(None, "tp"), P(None, "tp"), P("tp", None)),
        out_specs=P("dp", None),
        check_vma=False,
    )
```

time: 207 us -> 102 us (0.49)
  matrix products: 108 us -> 0 us
  Pallas kernels: 0 us -> 102 us
  waiting for transfers between devices: 78.6 us -> 0 us
  between operations: 13.4 us -> 0.01 us
  local copies, waits for them, and re-layouts: 5.72 us -> 0 us
    dot_general x3 -> x0, matrix products: 108 us -> none  [the longest x1 36.4 us: step(): jnp.dot(hidden, w_down, preferred_element_type=jnp.float32)]
    pallas_call x0 -> x2, Pallas kernels: none -> 102 us  [the longest x1 98.8 us: step(): pl.pallas_call(functools.partial(kernel, rows, depth, units, kc, cw), out...]
    psum x1 -> x0, waiting for transfers between devices: 78.6 us -> none  [step(): return lax.psum(term, 'tp')]
    unnamed x3 -> x0, local copies, waits for them, and re-layouts: 5.72 us -> none
  transfers between devices with their start and end apart: 1 -> 0, of which waited for: 1 -> 0; matrix products, arithmetic and copies ran while one was open for 0% -> 0% of each run, Pallas kernels for 0% -> 0%
where the time goes in v2:
time: 102 us
  Pallas kernels  102 us (100%)
    pallas_call x1, Pallas kernels, step(): pl.pallas_call(functools.partial(kernel, rows, depth, units, kc, cw), out...  98.8 us
    pallas_call x1, Pallas kernels, step(): pl.pallas_call(hand_on, out_shape=jax.ShapeDtypeStruct((rows, depth), BF1...  2.8 us

profile of v2, /device:TPU:1, one launch (start us, length us, event | category | flops | bytes accessed | tf_op | source)
XLA Modules:
  0.0 101.7 jit_solution(10563286808785234737)
XLA Ops:
  0.0 98.8 %shard_map.46.y_hbm = bf16[128,12288]{1,0:T(8,128)(2,1)} custom-call(bf16[128,12288]{1,0:T(8,128)(2,1)} %x_hbm.1, bf16[12288,4224]{1,0:T(8,128)(2,1)} %wg_hbm.1, bf16[12288,4224]{1,0:T(8,128)(2,1)} %wu_hbm.1, bf16[4224,12288]{1,0:T(8,128)(2,1)} %wd_hbm.1), custom_call_target="tpu_custom_call" | custom-call | tf_op jit(solution)/shard_map/pallas_call | solution.py:418
  98.9 2.8 %shard_map.47 = bf16[128,12288]{1,0:T(8,128)(2,1)} custom-call(bf16[128,12288]{1,0:T(8,128)(2,1)} %shard_map.46.y_hbm), custom_call_target="tpu_custom_call" | custom-call | tf_op jit(solution)/shard_map/pallas_call | solution.py:451

commit v3 on v2

--- a/solution.py
+++ b/solution.py
@@ -12,21 +12,20 @@
 LANES = 128
 
 KC = 512
-NS = 6
-DIRECT = 2
+NS = 8
 CW = 512
 SPLIT = 2
-ND = 4
+ND = 2
 LD, LX, LE, LR, LG = 1, 4, 6, 9, 13
 
-PARTS = 6
+PARTS = 8
 
 
 def kernel(
     rows, depth, units, kc, cw,
     x_hbm, wg_hbm, wu_hbm, wd_hbm, y_hbm,
     xs, wbuf, acc, hid, dbuf, d_in, x_in, e_in, r_in, yv,
-    xl_sem, w_sem, wd_sem, y_sem, send_sem, xa_sem, xz_sem, xb_sem, d_sem, x_sem, z_sem, y_in_sem,
+    xl_sem, w_sem, wd_sem, y_sem, send_sem, xa_sem, xb_sem, d_sem, x_sem, z_sem, y_in_sem,
 ):
     dp, tp = lax.axis_index("dp"), lax.axis_index("tp")
     z, core = tp // 2, tp % 2
@@ -35,8 +34,7 @@
     partner = tp + 1 - 2 * core
     is_end = (z == 0) | (z == 3)
     is_mid = (z == 1) | (z == 2)
-    odd = z % 2
-    tp_pair = tp + 2 - 4 * odd
+    tp_pair = tp + 2 - 4 * (z % 2)
     tp_far = (3 - z) * 2 + core
 
     nk, nch = depth // kc, depth // cw
@@ -47,7 +45,7 @@
     hc = cw // 2
     sc = hc // SPLIT
     ring = 2 * width // hc
-    own, oth, both = pl.ds(0, rows), pl.ds(rows, rows), pl.ds(0, 2 * rows)
+    own, oth = pl.ds(0, rows), pl.ds(rows, rows)
 
     def weights(k):
         slot = lax.rem(k, NS)
@@ -77,24 +75,13 @@
     def x_half(k, c):
         return pl.ds(pl.multiple_of(k * kc + c * (kc // 2), LANES), kc // 2)
 
-    def x_quarter(k, q):
-        return pl.ds(pl.multiple_of(k * kc + core * (kc // 2) + q * (kc // 4), LANES), kc // 4)
-
     def x_whole(k):
         c = x_half(k, core)
         return send(xs.at[own, c], xs.at[oth, c], 0, xa_sem.at[k], dp=across)
 
-    def x_part(k):
-        c = x_quarter(k, odd)
-        return send(xs.at[own, c], xs.at[oth, c], 0, xa_sem.at[k], dp=across)
-
-    def x_pair(k, q):
-        c = x_quarter(k, q)
-        return send(xs.at[oth, c], xs.at[oth, c], 1, xz_sem.at[k], tp=tp_pair)
-
     def x_partner(k, c):
         c = x_half(k, c)
-        return send(xs.at[oth, c], xs.at[oth, c], 2, xb_sem.at[k], tp=partner)
+        return send(xs.at[oth, c], xs.at[oth, c], 1, xb_sem.at[k], tp=partner)
 
     def d_out(n):
         return wbuf.at[0, pl.ds((n % 2) * 256, 2 * rows), pl.ds(pl.multiple_of((n // 2) * hc, hc), hc)]
@@ -162,13 +149,9 @@
     def _():
         pl.semaphore_wait(barrier, 4)
 
-    @pl.loop(0, DIRECT)
+    @pl.loop(0, nk)
     def _(k):
         x_whole(k).start()
-
-    @pl.loop(DIRECT, nk)
-    def _(k):
-        x_part(k).start()
 
     @pl.loop(0, 2 * wt)
     def _(j):
@@ -185,40 +168,8 @@
                 xs[r, kb], wbuf[b, :, out], preferred_element_type=F32
             )
 
-        for t in range(0, 2 * wt - 2, 2):
+        for t in range(0, 2 * wt, 2):
             tile(r, t)
-        if r is both:
-            tile(own, 2 * wt - 2)
-            tile(oth, 2 * wt - 2)
-        else:
-            tile(r, 2 * wt - 2)
-
-    def to_pair(k):
-        k = jnp.int32(k)
-
-        @pl.when((k >= DIRECT) & (k < nk))
-        def _():
-            x_part(k).wait_recv()
-            x_pair(k, odd).start()
-
-    def to_partner(k):
-        k = jnp.int32(k)
-
-        @pl.when(k < DIRECT)
-        def _():
-            x_whole(k).wait_recv()
-
-        @pl.when((k >= DIRECT) & (k < nk))
-        def _():
-            x_pair(k, 1 - odd).wait_recv()
-
-        @pl.when(k < nk)
-        def _():
-            x_partner(k, core).start()
-
-    def pieces(i, per):
-        for j in range(2):
-            per(2 * i + j)
 
     def refill(i):
         for j in range(2):
@@ -234,45 +185,31 @@
                 for c in down(k - nk):
                     c.start()
 
-    def early(i, r):
-        for k in (2 * i, 2 * i + 1):
-            if r is own:
-                for c in weights(k):
-                    c.wait()
-                if i == 0:
-                    for c in weights(k + 4):
-                        c.start()
-            else:
-                x_partner(k, 1 - core).wait_recv()
-        project(i, r)
-        if r is oth:
-            refill(i)
-
-    early(0, own)
-    early(1, own)
-    pieces(0, to_partner)
-    pieces(1, to_pair)
-    early(2, own)
-    pieces(2, to_pair)
-    early(0, oth)
-    pieces(3, to_pair)
-    pieces(1, to_partner)
-    pieces(4, to_pair)
-    pieces(2, to_partner)
-    early(1, oth)
-    pieces(5, to_pair)
-    pieces(3, to_partner)
-    early(2, oth)
-
-    @pl.loop(3, nk // 2)
-    def _(i):
-        pieces(i + 3, to_pair)
-        pieces(i + 1, to_partner)
+    def arrived(i):
         for j in range(2):
             for c in weights(2 * i + j):
                 c.wait()
+
+    arrived(0)
+    for k in range(4, NS):
+        for c in weights(k):
+            c.start()
+    project(0, own)
+
+    @pl.loop(0, nk // 2)
+    def _(i):
+        for j in range(2):
+            x_whole(2 * i + j).wait_recv()
+            x_partner(2 * i + j, core).start()
+
+        @pl.when(i + 1 < nk // 2)
+        def _():
+            arrived(i + 1)
+            project(i + 1, own)
+
+        for j in range(2):
             x_partner(2 * i + j, 1 - core).wait_recv()
-        project(i, both)
+        project(i, oth)
         refill(i)
 
     @pl.loop(0, wt)
@@ -378,9 +315,8 @@
         ref = yv.at[:, pl.ds(0, columns)]
         send(ref, ref, kind, xl_sem, tp=partner).wait_send()
 
-    drain(0, DIRECT * (kc // 2) + (nk - DIRECT) * (kc // 4))
-    drain(1, (nk - DIRECT) * (kc // 4))
-    drain(2, depth // 2)
+    drain(0, depth // 2)
+    drain(1, depth // 2)
     drain(3, depth)
     drain(4, depth // 2)
     drain(5, depth // 2)
@@ -438,7 +374,6 @@
                 dma((8,)),
                 dma((nk,)),
                 dma((nk,)),
-                dma((nk,)),
                 dma((nch,)),
                 dma((nch * SPLIT,)),
                 dma((2, nch * SPLIT)),

time: 102 us -> 100 us (0.980)
  Pallas kernels: 102 us -> 99.9 us
    pallas_call x1, Pallas kernels: 98.8 us -> 97.1 us  [step(): pl.pallas_call(functools.partial(kernel, rows, depth, units, kc, cw), out...]
where the time goes in v3:
time: 100 us; the launch traced here: 99.9 us
  Pallas kernels  99.9 us (100%)
    pallas_call x1, Pallas kernels, step(): pl.pallas_call(functools.partial(kernel, rows, depth, units, kc, cw), out...  97.1 us
    pallas_call x1, Pallas kernels, step(): pl.pallas_call(hand_on, out_shape=jax.ShapeDtypeStruct((rows, depth), BF1...  2.79 us

profile of v3, /device:TPU:1, one launch (start us, length us, event | category | flops | bytes accessed | tf_op | source)
XLA Modules:
  0.0 99.9 jit_solution(6879685371294169254)
XLA Ops:
  0.0 97.1 %shard_map.46.y_hbm = bf16[128,12288]{1,0:T(8,128)(2,1)} custom-call(bf16[128,12288]{1,0:T(8,128)(2,1)} %x_hbm.1, bf16[12288,4224]{1,0:T(8,128)(2,1)} %wg_hbm.1, bf16[12288,4224]{1,0:T(8,128)(2,1)} %wu_hbm.1, bf16[4224,12288]{1,0:T(8,128)(2,1)} %wd_hbm.1), custom_call_target="tpu_custom_call" | custom-call | tf_op jit(solution)/shard_map/pallas_call | solution.py:354
  97.1 2.8 %shard_map.47 = bf16[128,12288]{1,0:T(8,128)(2,1)} custom-call(bf16[128,12288]{1,0:T(8,128)(2,1)} %shard_map.46.y_hbm), custom_call_target="tpu_custom_call" | custom-call | tf_op jit(solution)/shard_map/pallas_call | solution.py:386
